TPU v7x, 32 devices: a whole 2x2x4 slice. The times are simulated.
32 devices in a mesh: ep: 2 (over y), tp: 16 (over z, x, core).
Axes of the slice: x: 2, y: 2, z: 4, core: 2. Of those that a mesh axis runs over, the one named last changes fastest.
Arguments:
- activations: bfloat16 [64, 6144], P(None, 'tp'), may hold values from -6 to 6
- norm_gain: float32 [6144], replicated, may hold values from 0.1 to 1.9
- router_weight: bfloat16 [6144, 8], P('tp'), may hold values from -0.078125 to 0.078125
- expert_ids: int32 [64, 2], replicated, may hold values from 0 to 7, all different within a row
- w_gate: bfloat16 [8, 6144, 2048], P('ep', None, 'tp'), may hold values from -0.078125 to 0.078125
- w_up: bfloat16 [8, 6144, 2048], P('ep', None, 'tp'), may hold values from -0.078125 to 0.078125
- w_down: bfloat16 [8, 2048, 6144], P('ep', 'tp'), may hold values from -0.1875 to 0.1875
Outputs:
- moe_out: bfloat16 [64, 6144], P(None, 'tp')
Inputs may be any that keep to these rules, and one draw needn't show every extreme that they name: `expert_ids`: each row names two different experts from 0 to 7, and every expert is named by some token.
All inputs are finite; a program needn't handle non-finite values.
Results may differ from a plain program's by a relative error of at most 0.0025.
Values may be sent and summed in bfloat16 or wider, within the bound.
A program may use at most 64 MiB of HBM per device.

v0:
```python
import jax
import jax.numpy as jnp
from jax import lax
from jax.sharding import PartitionSpec as P

epsilon = 1e-05


def summed_rows(portion, rows, axis):
    count = rows * lax.axis_size(axis)
    return lax.psum_scatter(portion(jnp.int32(0), count), axis, scatter_dimension=0, tiled=True)


def shards(activations, norm_gain, router_weight, expert_ids, w_gate, w_up, w_down):
    shard_width = activations.shape[1]
    gathered = lax.all_gather(activations, "tp", axis=1, tiled=True)
    features = gathered.astype(jnp.float32)
    inv_rms = lax.rsqrt(jnp.mean(features * features, axis=1, keepdims=True) + epsilon)
    normed = (features * inv_rms * norm_gain.astype(jnp.float32)).astype(jnp.bfloat16)
    router_full = lax.all_gather(router_weight, "tp", axis=0, tiled=True)
    logits = jnp.dot(normed, router_full, preferred_element_type=jnp.float32)
    expert_total = router_weight.shape[1]
    chosen = jnp.take_along_axis(logits, expert_ids, axis=1)
    weights = jax.nn.softmax(chosen, axis=1)
    gate_dense = jnp.sum(
        weights[:, :, None] * jax.nn.one_hot(expert_ids, expert_total, dtype=jnp.float32), axis=1
    )
    local_count = w_gate.shape[0]
    local_gates = lax.dynamic_slice_in_dim(
        gate_dense, lax.axis_index("ep") * local_count, local_count, 1
    )
    gate_per_expert = local_gates.T
    gate_act = jnp.einsum("td,edf->etf", normed, w_gate, preferred_element_type=jnp.float32)
    up_act = jnp.einsum("td,edf->etf", normed, w_up, preferred_element_type=jnp.float32)
    hidden = (jax.nn.silu(gate_act) * up_act).astype(jnp.bfloat16)

    def weighted_terms(begin_row, row_count):
        columns = lax.dynamic_slice_in_dim(w_down, begin_row, row_count, 2)
        products = jnp.einsum("efc,etf->ect", columns, hidden, preferred_element_type=jnp.float32)
        return jnp.sum(products * gate_per_expert[:, None, :], axis=0)

    own_rows = summed_rows(weighted_terms, shard_width, "tp")
    summed = lax.psum(own_rows, "ep")
    return summed.T.astype(jnp.bfloat16)


def solution(mesh):
    in_specs = (
        P(None, "tp"),
        P(),
        P("tp", None),
        P(),
        P("ep", None, "tp"),
        P("ep", None, "tp"),
        P("ep", "tp", None),
    )
    out_specs = P(None, "tp")
    return jax.shard_map(shards, mesh=mesh, in_specs=in_specs, out_specs=out_specs, check_vma=False)
```

profile of v0, /device:TPU:0, one launch (start us, length us, event | category | flops | bytes accessed | tf_op | source)
XLA Modules:
  0.0 141.2 jit_solution(3283291192828274340)
XLA Ops:
  6.5 0.0 copy-start
  6.5 0.0 reduce-scatter.2.cloned.1.call-start
  6.5 0.7 bitcast_or_fusion
  7.2 0.1 copy.32
  7.3 0.1 reshape.41
  7.5 23.6 %all_gather.7 = bf16[6144,8]{0,1:T(8,128)(2,1)S(1)} all-gather(bf16[384,8]{0,1:T(8,128)(2,1)} %param.9), channel_id=1, replica_groups=mesh['ep'=2,'tp'=16] {'tp'}, dimensions={0}, use_global_device_ids=true | all-gather | bytes 104448 | tf_op jit(solution)/shard_map/all_gather | solution.py:20
  31.1 19.8 %all_gather.6 = bf16[64,6144]{1,0:T(8,128)(2,1)S(1)} all-gather(bf16[64,384]{1,0:T(8,128)(2,1)} %param.7), channel_id=1, replica_groups=mesh['ep'=2,'tp'=16] {'tp'}, dimensions={1}, use_global_device_ids=true | all-gather | bytes 835584 | tf_op jit(solution)/shard_map/all_gather | solution.py:16
  50.9 0.3 fusion.1
  51.2 0.0 copy-done
  51.2 0.4 fusion.21
  51.6 0.0 copy-start.1
  51.6 1.0 gather_fusion
  52.6 0.1 reshape.44
  52.7 0.1 copy.33
  52.8 0.0 copy-done.1
  52.9 4.0 %convolution_bitcast_fusion.1 = f32[4,64,128]{2,1,0:T(8,128)S(1)} fusion(bf16[4,6144,128]{2,1,0:T(8,128)(2,1)} %param.11, bf16[64,6144]{1,0:T(8,128)(2,1)S(1)} %all_gather.6, f32[6144]{0:T(1024)S(1)} %copy-done, f32[64]{0:T(128)S(1)} %add_rsqrt_fusion), kind=kOutput, calls=%fused_computation.10 | convolution fusion | flops 404226048 | bytes 7233792 | tf_op jit(solution)/shard_map/td,edf->etf/dot_general | solution.py:33
  57.0 8.7 %fusion = f32[64,6144]{1,0:T(8,128)} fusion(f32[4,64]{1,0:T(4,128)S(1)} %dynamic-slice_bitcast_fusion, bf16[4,128,6144]{2,1,0:T(8,128)(2,1)} %param.13, bf16[4,6144,128]{2,1,0:T(8,128)(2,1)} %param.12, f32[4,64,128]{2,1,0:T(8,128)S(1)} %convolution_bitcast_fusion.1, bf16[64,6144]{1,0:T(8,128)(2,1)S(1)} %all_gather.6, f32[6144]{0:T(1024)S(1)} %copy-done, ...), kind=kOutput, calls=%fused_computation.2 | convolution fusion | flops 809828352 | bytes 15099136 | tf_op jit(solution)/shard_map/efc,etf->ect/dot_general | solution.py:39
  65.7 0.0 reduce-scatter.2.cloned.1.call-update
  65.7 58.2 %reduce-scatter.2.cloned.1.call-done = f32[384,64]{0,1:T(8,128)} async-done(((f32[6144,64]{0,1:T(8,128)}), f32[384,64]{0,1:T(8,128)}) %reduce-scatter.2.cloned.1.call-update) | async-done | bytes 98320 | tf_op jit(solution)/shard_map/reduce_scatter | solution.py:11
  123.9 10.4 %psum.7 = bf16[384,64]{0,1:T(8,128)(2,1)} all-reduce(f32[384,64]{0,1:T(8,128)} %reduce-scatter.2.cloned.1.call-done), channel_id=1, replica_groups=mesh['ep'=2,'tp'=16] {'ep'}, use_global_device_ids=true, to_apply=%region_6.7 | all-reduce | flops 24576 | bytes 147456 | tf_op jit(solution)/shard_map/psum | solution.py:43
  (6 shorter events, 0.1 us)
Async XLA Ops:
  6.5 44.6 %copy-start = (f32[6144]{0:T(1024)S(1)}, f32[6144]{0:T(1024)}, u32[]{:S(2)}) copy-start(f32[6144]{0:T(1024)} %param.8) | copy-start | bytes 73732
  6.5 117.3 %reduce-scatter.2.cloned.1.call-start = ((), (), s32[]{:S(2)}) async-start(), calls=%async_computation.1 | async-start | bytes 1671168 | tf_op jit(solution)/shard_map/reduce_scatter | solution.py:11
  51.6 1.2 copy-start.1
Sparse Core Ops, SparseCore 0:
  65.8 57.9 reduce-scatter.1
where the time goes:
time: 141 us
  waiting for transfers between devices  58.2 us (41%)
  blocking collectives  53.9 us (38%)
  between operations  13.5 us (10%)
  matrix products  13.2 us (9%)
  local copies, waits for them, and re-layouts  1.47 us (1%)
    reduce_scatter x1, waiting for transfers between devices, summed_rows(): lax.psum_scatter(portion(jnp.int32(0), count), axis, scatter_dimension=0,...  58.2 us
    all_gather x1, blocking collectives, shards(): router_full = lax.all_gather(router_weight, 'tp', axis=0, tiled=True)  23.6 us
    all_gather x1, blocking collectives, shards(): gathered = lax.all_gather(activations, 'tp', axis=1, tiled=True)  19.8 us
    psum x1, blocking collectives, shards(): summed = lax.psum(own_rows, 'ep')  10.4 us
    dot_general x1, matrix products, weighted_terms(): jnp.einsum('efc,etf->ect', columns, hidden, preferred_element_type=jnp.fl...  8.72 us
    dot_general x1, matrix products, shards(): jnp.einsum('td,edf->etf', normed, w_gate, preferred_element_type=jnp.floa...  4.05 us
  transfers between devices with their start and end apart: 1, of which 1 were waited for; matrix products, arithmetic and copies ran while one was open for 0% of the time, Pallas kernels for 0%

commit v1 on v0

--- a/solution.py
+++ b/solution.py
@@ -13,7 +13,7 @@
 
 def shards(activations, norm_gain, router_weight, expert_ids, w_gate, w_up, w_down):
     shard_width = activations.shape[1]
-    gathered = lax.all_gather(activations, "tp", axis=1, tiled=True)
+    gathered = jnp.concatenate(lax.all_gather(activations, "tp"), axis=1)
     features = gathered.astype(jnp.float32)
     inv_rms = lax.rsqrt(jnp.mean(features * features, axis=1, keepdims=True) + epsilon)
     normed = (features * inv_rms * norm_gain.astype(jnp.float32)).astype(jnp.bfloat16)

time: 141 us -> 141 us (level)
  no operation moved by 1% of the time
where the time goes in v1:
time: 141 us
  waiting for transfers between devices  58.2 us (41%)
  blocking collectives  53.8 us (38%)
  between operations  13.5 us (10%)
  matrix products  12.7 us (9%)
  local copies, waits for them, and re-layouts  1.59 us (1%)
  other arithmetic  1.41 us (1%)
    reduce_scatter x1, waiting for transfers between devices, summed_rows(): lax.psum_scatter(portion(jnp.int32(0), count), axis, scatter_dimension=0,...  58.2 us
    all_gather x1, blocking collectives, shards(): router_full = lax.all_gather(router_weight, 'tp', axis=0, tiled=True)  23.6 us
    all_gather x1, blocking collectives, shards(): gathered = jnp.concatenate(lax.all_gather(activations, 'tp'), axis=1)  19.8 us
    psum x1, blocking collectives, shards(): summed = lax.psum(own_rows, 'ep')  10.4 us
    dot_general x1, matrix products, weighted_terms(): jnp.einsum('efc,etf->ect', columns, hidden, preferred_element_type=jnp.fl...  8.38 us
    dot_general x1, matrix products, shards(): jnp.einsum('td,edf->etf', normed, w_gate, preferred_element_type=jnp.floa...  3.98 us
  transfers between devices with their start and end apart: 1, of which 1 were waited for; matrix products, arithmetic and copies ran while one was open for 0% of the time, Pallas kernels for 0%

profile of v1, /device:TPU:0, one launch (start us, length us, event | category | flops | bytes accessed | tf_op | source)
XLA Modules:
  0.0 141.2 jit_solution(10882061911294789257)
XLA Ops:
  6.5 0.0 copy-start
  6.5 0.0 reduce-scatter.2.cloned.1.call-start
  6.5 0.7 bitcast_or_fusion
  7.2 0.1 copy.36
  7.3 0.1 reshape.46
  7.5 23.6 %all_gather.11 = bf16[6144,8]{0,1:T(8,128)(2,1)S(1)} all-gather(bf16[384,8]{0,1:T(8,128)(2,1)} %param.9), channel_id=1, replica_groups=mesh['ep'=2,'tp'=16] {'tp'}, dimensions={0}, use_global_device_ids=true | all-gather | bytes 104448 | tf_op jit(solution)/shard_map/all_gather | solution.py:20
  31.1 19.8 %all-gather = bf16[1024,384]{1,0:T(8,128)(2,1)S(1)} all-gather(bf16[64,384]{1,0:T(8,128)(2,1)} %param.7), channel_id=2, replica_groups=mesh['ep'=2,'tp'=16] {'tp'}, dimensions={0}, use_global_device_ids=true | all-gather | bytes 835584 | tf_op jit(solution)/shard_map/all_gather | solution.py:16
  50.9 0.2 convert_bitcast_fusion
  51.1 0.3 fusion.1
  51.3 0.1 copy.38
  51.5 0.0 copy-done
  51.5 0.2 multiply_convert_fusion
  51.7 0.3 fusion.18
  52.0 0.0 copy-start.1
  52.0 1.0 gather_fusion
  53.0 0.1 reshape.49
  53.2 0.1 copy.37
  53.2 0.0 copy-done.1
  53.3 4.0 %convolution_bitcast_fusion.1 = f32[4,64,128]{2,1,0:T(8,128)S(1)} fusion(bf16[4,6144,128]{2,1,0:T(8,128)(2,1)} %param.11, bf16[64,6144]{1,0:T(8,128)(2,1)S(1)} %multiply_convert_fusion), kind=kOutput, calls=%fused_computation.9 | convolution fusion | flops 402653184 | bytes 7208960 | tf_op jit(solution)/shard_map/td,edf->etf/dot_general | solution.py:33
  57.3 8.4 %fusion = f32[64,6144]{1,0:T(8,128)} fusion(f32[4,64]{1,0:T(4,128)S(1)} %dynamic-slice_bitcast_fusion, bf16[4,128,6144]{2,1,0:T(8,128)(2,1)} %param.13, bf16[4,6144,128]{2,1,0:T(8,128)(2,1)} %param.12, bf16[64,6144]{1,0:T(8,128)(2,1)S(1)} %multiply_convert_fusion, f32[4,64,128]{2,1,0:T(8,128)S(1)} %convolution_bitcast_fusion.1), kind=kOutput, calls=%fused_computation.2 | convolution fusion | flops 808255488 | bytes 15074304 | tf_op jit(solution)/shard_map/efc,etf->ect/dot_general | solution.py:39
  65.7 0.0 reduce-scatter.2.cloned.1.call-update
  65.7 58.2 %reduce-scatter.2.cloned.1.call-done = f32[384,64]{0,1:T(8,128)} async-done(((f32[6144,64]{0,1:T(8,128)}), f32[384,64]{0,1:T(8,128)}) %reduce-scatter.2.cloned.1.call-update) | async-done | bytes 98320 | tf_op jit(solution)/shard_map/reduce_scatter | solution.py:11
  123.9 10.4 %psum.7 = bf16[384,64]{0,1:T(8,128)(2,1)} all-reduce(f32[384,64]{0,1:T(8,128)} %reduce-scatter.2.cloned.1.call-done), channel_id=1, replica_groups=mesh['ep'=2,'tp'=16] {'ep'}, use_global_device_ids=true, to_apply=%region_6.7 | all-reduce | flops 24576 | bytes 147456 | tf_op jit(solution)/shard_map/psum | solution.py:43
  (6 shorter events, 0.1 us)
Async XLA Ops:
  6.5 44.9 %copy-start = (f32[6144]{0:T(1024)S(1)}, f32[6144]{0:T(1024)}, u32[]{:S(2)}) copy-start(f32[6144]{0:T(1024)} %param.8) | copy-start | bytes 73732
  6.5 117.4 %reduce-scatter.2.cloned.1.call-start = ((), (), s32[]{:S(2)}) async-start(), calls=%async_computation.1 | async-start | bytes 1671168 | tf_op jit(solution)/shard_map/reduce_scatter | solution.py:11
  52.0 1.2 copy-start.1
Sparse Core Ops, SparseCore 0:
  65.9 58.0 reduce-scatter.1
